TPU v7x, 128 devices: a whole 4x4x4 slice. The times are simulated.
128 devices in a mesh: seq: 8 (over z, core), exp: 16 (over y, x).
Axes of the slice: x: 4, y: 4, z: 4, core: 2. Of those that a mesh axis runs over, the one named last changes fastest.
Arguments:
- tokens: bfloat16 [81920, 4096], P(('seq', 'exp')), may hold values from -6 to 6
- routes: int32 [81920, 2], P(('seq', 'exp')), may hold values from 0 to 31, all different within a row; in each aligned block of 640 rows (0 to 639, 640 to 1279, ...) at most 50 rows name the same one
- gates: float32 [81920, 2], P(('seq', 'exp')), may hold values from 0.1 to 1
- weights: bfloat16 [32, 4096, 1024], P('exp', 'seq'), may hold values from -0.09375 to 0.09375
Outputs:
- mixed: bfloat16 [81920, 1024], P(('seq', 'exp'))
Inputs may be any that keep to these rules, and one draw needn't show every extreme that they name: `routes`: the two experts of a token differ. Among the rows of one device no expert is named more than 50 times, a bound that some block reaches.
All inputs are finite; a program needn't handle non-finite values.
Results may differ from a plain program's by a relative error of at most 0.0049.
Values may be sent and summed in bfloat16 or wider, within the bound.
A program may use at most 192 MiB of HBM per device.

v0:
```python
import jax
import jax.numpy as jnp
from jax import lax
from jax.sharding import PartitionSpec as P


def route_slots(route_block, experts, capacity):
    expert_ids = route_block.reshape(-1)
    one_hot = (expert_ids[:, None] == jnp.arange(experts, dtype=jnp.int32)[None, :]).astype(
        jnp.int32
    )
    earlier = jnp.cumsum(one_hot, axis=0) - one_hot
    slot_index = jnp.sum(earlier * one_hot, axis=1)
    return expert_ids * capacity + slot_index


def body(tokens, routes, gates, weights):
    groups = lax.axis_size("exp")
    per_group = weights.shape[0]
    experts = per_group * groups
    count_rows = tokens.shape[0]
    width = tokens.shape[1]
    capacity = 5 * count_rows // (2 * experts)
    position = route_slots(routes, experts, capacity)
    local_rows = jnp.arange(2 * count_rows, dtype=jnp.int32) // 2
    slot_rows = jnp.full((experts * capacity,), count_rows, jnp.int32).at[position].set(local_rows)
    padded = jnp.concatenate([tokens, jnp.zeros((1, width), jnp.bfloat16)], axis=0)
    outgoing = padded[slot_rows].reshape(groups, per_group, capacity, width)
    whole_weights = lax.all_gather(weights, "seq", axis=1, tiled=True)
    returned = lax.all_to_all(
        jnp.einsum(
            "sjcd,jdf->sjcf",
            lax.all_to_all(outgoing, "exp", split_axis=0, concat_axis=0, tiled=True),
            whole_weights,
            preferred_element_type=jnp.float32,
        ).astype(jnp.bfloat16),
        "exp",
        split_axis=0,
        concat_axis=0,
        tiled=True,
    )
    hidden = returned.shape[-1]
    results = returned.reshape(experts * capacity, hidden)
    picked = results[position].reshape(count_rows, 2, hidden).astype(jnp.float32)
    mixed = jnp.sum(picked * gates[:, :, None], axis=1)
    return mixed.astype(jnp.bfloat16)


def solution(mesh):
    return jax.shard_map(
        body,
        mesh=mesh,
        in_specs=(
            P(("seq", "exp"), None),
            P(("seq", "exp"), None),
            P(("seq", "exp"), None),
            P("exp", "seq", None),
        ),
        out_specs=P(("seq", "exp"), None),
        check_vma=False,
    )
```

profile of v0, /device:TPU:24, one launch (start us, length us, event | category | flops | bytes accessed | tf_op | source)
XLA Modules:
  0.0 390.5 jit_solution(17907543015240691202)
XLA Ops:
  6.5 0.7 all-gather.2.cloned.1.call-update
  7.3 0.9 copy.15
  8.1 0.2 eq.29
  8.3 0.2 eq.25
  8.6 9.1 %reduce-window.6 = s32[32,10,128]{2,1,0:T(8,128)S(1)} reduce-window(s32[32,10,128]{2,1,0:T(8,128)S(1)} %fusion.7, s32[]{:T(128)} %constant.29.clone.1), window={size=1x1x128 pad=0_0x0_0x127_0}, to_apply=%region_0.0 | reduce-window | flops 5201920 | bytes 327684 | tf_op jit(solution)/shard_map/reduce-window
  17.8 0.2 copy.17
  18.1 0.7 broadcast_multiply_fusion
  19.0 0.2 mul.29
  19.2 6.8 %concatenate.3 = bf16[641,4096]{1,0:T(8,128)(2,1)} pad(bf16[640,4096]{1,0:T(8,128)(2,1)} %param.4, bf16[]{:T(256)} %constant.26.clone.1), padding=0_1x0_0 | pad | bytes 10493954 | tf_op jit(solution)/shard_map/concatenate | solution.py:27
  26.2 5.2 %scatter_custom_fusion = s32[1600]{0:T(1024)S(1)} fusion(s32[1280]{0:T(1024)S(1)} %fusion.14, s32[1280]{0:T(1024)S(1)} %add_select_fusion, s32[]{:T(128)} %constant.27.clone.1), kind=kCustom, calls=%fused_computation.28 | custom fusion | bytes 6404 | tf_op jit(solution)/shard_map/scatter | solution.py:26
  31.5 28.1 %gather_fusion = bf16[1600,4096]{1,0:T(8,128)(2,1)} fusion(bf16[641,4096]{1,0:T(8,128)(2,1)} %concatenate.3, s32[2048]{0:T(1024)S(1)} %pad_clamp_fusion.1), kind=kCustom, calls=%fused_computation | custom fusion | bytes 26220800 | tf_op jit(solution)/shard_map/gather | solution.py:28
  59.6 13.3 %reshape.57 = bf16[16,2,50,4096]{3,2,1,0:T(8,128)(2,1)} reshape(bf16[1600,4096]{1,0:T(8,128)(2,1)} %gather_fusion) | data formatting | bytes 26214400 | tf_op jit(solution)/shard_map/reshape | solution.py:28
  72.9 19.4 %copy.19 = bf16[16,2,50,4096]{3,1,2,0:T(2,128)(2,1)S(1)} copy(bf16[16,2,50,4096]{3,2,1,0:T(8,128)(2,1)} %reshape.57) | data formatting | bytes 26214400 | tf_op jit(solution)/shard_map/reshape | solution.py:28
  92.3 151.2 %all_to_all.10 = bf16[16,2,50,4096]{3,1,2,0:T(2,128)(2,1)} all-to-all(bf16[16,2,50,4096]{3,1,2,0:T(2,128)(2,1)S(1)} %copy.19), channel_id=1, replica_groups=mesh['seq'=8,'exp'=16] {'exp'}, dimensions={0} | all-to-all | bytes 26214400 | tf_op jit(solution)/shard_map/all_to_all | solution.py:33
  243.5 53.3 %convert_bitcast_fusion = bf16[16,2,50,1024]{3,2,0,1:T(8,128)(2,1)} fusion(bf16[2,4096,1024]{2,1,0:T(8,128)(2,1)} %all-gather.2.cloned.1.call-done, bf16[16,2,50,4096]{3,1,2,0:T(2,128)(2,1)} %all_to_all.10), kind=kOutput, calls=%fused_computation.7 | convolution fusion | flops 13423411200 | bytes 33161216 | tf_op jit(solution)/shard_map/sjcd,jdf->sjcf/dot_general | solution.py:31
  296.8 7.1 %copy.21 = bf16[16,2,50,1024]{3,1,2,0:T(2,128)(2,1)} copy(bf16[16,2,50,1024]{3,2,0,1:T(8,128)(2,1)} %convert_bitcast_fusion) | data formatting | bytes 6553600 | tf_op jit(solution)/shard_map/convert_element_type | solution.py:36
  303.9 6.0 %all-to-all-start.1 = ((bf16[16,2,50,1024]{3,1,2,0:T(2,128)(2,1)}), bf16[16,2,50,1024]{3,1,2,0:T(2,128)(2,1)S(1)}, u32[]{:S(2)}, u32[]{:S(2)}) async-start(bf16[16,2,50,1024]{3,1,2,0:T(2,128)(2,1)} %copy.21), calls=%async_computation.1 | async-start | bytes 6553600 | tf_op jit(solution)/shard_map/all_to_all | solution.py:30
  309.9 0.9 copy.23
  310.8 44.5 %all-to-all-done.1 = bf16[16,2,50,1024]{3,1,2,0:T(2,128)(2,1)S(1)} async-done(((bf16[16,2,50,1024]{3,1,2,0:T(2,128)(2,1)}), bf16[16,2,50,1024]{3,1,2,0:T(2,128)(2,1)S(1)}, u32[]{:S(2)}, u32[]{:S(2)}) %all-to-all-start.1) | async-done | bytes 3276832 | tf_op jit(solution)/shard_map/all_to_all | solution.py:30
  355.3 3.0 copy.22
  358.2 3.2 reshape.58
  361.4 5.1 %gather_fusion.1 = bf16[1280,1024]{1,0:T(8,128)(2,1)} fusion(bf16[1600,1024]{1,0:T(8,128)(2,1)S(1)} %reshape.58, s32[2048]{0:T(1024)S(1)} %pad_clamp_fusion), kind=kCustom, calls=%fused_computation.1 | custom fusion | bytes 5248000 | tf_op jit(solution)/shard_map/gather | solution.py:44
  366.5 6.8 %reshape.59 = f32[640,2,1024]{2,1,0:T(2,128)} reshape(bf16[1280,1024]{1,0:T(8,128)(2,1)} %gather_fusion.1) | data formatting | bytes 7864320 | tf_op jit(solution)/shard_map/convert_element_type | solution.py:44
  373.3 10.3 %multiply_reduce_fusion = bf16[640,1024]{1,0:T(8,128)(2,1)} fusion(f32[640,2,1024]{2,1,0:T(2,128)} %reshape.59, f32[640,2]{1,0:T(8,128)S(1)} %copy-done), kind=kLoop, calls=%fused_computation.6 | loop fusion | flops 1966080 | bytes 6558720 | tf_op jit(solution)/shard_map/reduce_sum | solution.py:45
  (18 shorter events, 0.7 us)
Async XLA Ops:
  6.5 237.0 %all-gather.2.cloned.1.call-start = ((), (), s32[]{:S(2)}) async-start(), calls=%async_computation.2 | async-start | bytes 18874368 | tf_op jit(solution)/shard_map/all_gather | solution.py:29
  296.8 13.1 %copy-start.1 = (f32[640,2]{0,1:T(2,128)S(1)}, f32[640,2]{0,1:T(2,128)}, u32[]{:S(2)}) copy-start(f32[640,2]{0,1:T(2,128)} %param.6) | copy-start | bytes 15364
  303.9 51.4 %all-to-all-start.1 = ((bf16[16,2,50,1024]{3,1,2,0:T(2,128)(2,1)}), bf16[16,2,50,1024]{3,1,2,0:T(2,128)(2,1)S(1)}, u32[]{:S(2)}, u32[]{:S(2)}) async-start(bf16[16,2,50,1024]{3,1,2,0:T(2,128)(2,1)} %copy.21), calls=%async_computation.1 | async-start | bytes 6553600 | tf_op jit(solution)/shard_map/all_to_all | solution.py:30
  366.5 6.8 %copy-start = (f32[640,2]{1,0:T(8,128)S(1)}, f32[640,2]{1,0:T(8,128)}, u32[]{:S(2)}) copy-start(f32[640,2]{1,0:T(8,128)} %copy.23) | copy-start | bytes 15364
Sparse Core Ops, SparseCore 0:
  9.0 87.2 all-gather.1
where the time goes:
time: 393 us; the launch traced here: 390 us
  blocking collectives  151 us (38%)
  local copies, waits for them, and re-layouts  101 us (26%)
  matrix products  53.3 us (14%)
  waiting for transfers between devices  45.2 us (12%)
  other arithmetic  20.4 us (5%)
  between operations  13.5 us (3%)
  starting transfers between devices  5.99 us (2%)
    all_to_all x1, blocking collectives, body(): lax.all_to_all(outgoing, 'exp', split_axis=0, concat_axis=0, tiled=True)  151 us
    dot_general x1, matrix products, body(): jnp.einsum('sjcd,jdf->sjcf', lax.all_to_all(outgoing, 'exp', split_axis=0...  53.3 us
    all_to_all x1, waiting for transfers between devices, body(): lax.all_to_all(jnp.einsum('sjcd,jdf->sjcf', lax.all_to_all(outgoing, 'exp...  44.5 us
    reshape x2, local copies, waits for them, and re-layouts, body(): outgoing = padded[slot_rows].reshape(groups, per_group, capacity, width)  32.7 us
    gather x1, local copies, waits for them, and re-layouts, body(): outgoing = padded[slot_rows].reshape(groups, per_group, capacity, width)  28.1 us
    reduce_sum x1, other arithmetic, body(): mixed = jnp.sum(picked * gates[:, :, None], axis=1)  10.3 us
    another operation x3, other arithmetic  9.23 us
  transfers between devices with their start and end apart: 2, of which 1 were waited for; matrix products, arithmetic and copies ran while one was open for 22% of the time, Pallas kernels for 0%

commit v1 on v0

v1 whole, which is shorter than its diff:
```python
import functools

import jax
import jax.numpy as jnp
from jax import lax
from jax.experimental import pallas as pl
from jax.experimental.pallas import tpu as pltpu
from jax.sharding import PartitionSpec as P

GROUP = 4
TILE = 8


def shift_order(side):
    if side == 4:
        return [
            (2, 2), (1, 1), (3, 3), (2, 0),
            (1, 2), (3, 2), (2, 1), (0, 3),
            (2, 3), (1, 3), (3, 1), (0, 2),
            (1, 0), (3, 0), (0, 1), (0, 0),
        ]
    all_shifts = [(a, b) for a in range(side) for b in range(side)]
    return all_shifts[1:] + all_shifts[:1]


def kernel(side, depth_z, cap, tok, routes, routes_t, gates, w, out,
           send, recv, wfull, rr, oh, xbuf, acc,
           xsem, tsend, trecv, rsend, rrecv, wloc, wsend, wrecv):
    count, width = tok.shape
    hidden = w.shape[2]
    shard = w.shape[1]
    peers = side * side
    rows = 2 * cap
    padded = send.shape[1]
    experts = 2 * peers
    sent = -(-rows // TILE) * TILE
    groups = peers // GROUP
    chunks = 4
    chunk = width // chunks
    f32, bf16 = jnp.float32, jnp.bfloat16

    seq = lax.axis_index("seq")
    exp = lax.axis_index("exp")
    z, core = seq // 2, lax.rem(seq, 2)
    y, x = exp // side, lax.rem(exp, side)
    sibling = 2 * z + 1 - core
    shifts = shift_order(side)

    def there(i):
        return lax.rem(y + shifts[i][0], side) * side + lax.rem(x + shifts[i][1], side)

    def back(i):
        return (lax.rem(y - shifts[i][0] + side, side) * side
                + lax.rem(x - shifts[i][1] + side, side))

    def z_peer(dz):
        return 2 * lax.rem(z + dz, depth_z) + core

    own_rows = pl.ds(pl.multiple_of(seq * shard, shard), shard)
    local_w = pltpu.make_async_copy(w, wfull.at[:, own_rows, :], wloc)
    local_w.start()

    def x_copy(c):
        return pltpu.make_async_copy(
            tok.at[:, pl.ds(c * chunk, chunk)], xbuf.at[c % 2], xsem.at[c % 2])

    x_copy(0).start()
    x_copy(1).start()

    barrier = pltpu.get_barrier_semaphore()
    for i in range(peers - 1):
        pl.semaphore_signal(barrier, inc=1, device_id={"exp": there(i)})
    for dz in range(1, depth_z):
        pl.semaphore_signal(barrier, inc=1, device_id={"seq": z_peer(dz)})
    pl.semaphore_signal(barrier, inc=1, device_id={"seq": sibling})

    ra, rb = routes_t[0:1, :], routes_t[1:2, :]
    names = lax.broadcasted_iota(jnp.int32, (experts, count), 0)
    hit_a, hit_b = names == ra, names == rb
    both = jnp.where(hit_a | hit_b, 1.0, 0.0).astype(bf16)
    earlier = jnp.where(
        lax.broadcasted_iota(jnp.int32, (count, count), 0)
        < lax.broadcasted_iota(jnp.int32, (count, count), 1), 1.0, 0.0).astype(bf16)
    table = (jnp.dot(both, earlier, preferred_element_type=f32)
             + (names * cap).astype(f32))
    pos_a = jnp.sum(jnp.where(hit_a, table, 0.0), axis=0, keepdims=True)
    pos_b = jnp.sum(jnp.where(hit_b, table, 0.0), axis=0, keepdims=True)

    for i in range(peers):
        r = lax.broadcasted_iota(jnp.int32, (padded, count), 0)
        target = jnp.where(r < rows, (r + rows * there(i)), -1).astype(f32)
        hit = (pos_a == target) | (pos_b == target)
        oh[i * padded:(i + 1) * padded, :] = jnp.where(hit, 1.0, 0.0).astype(bf16)

    pl.semaphore_wait(barrier, peers - 1 + depth_z - 1 + 1)

    def w_copy(n, zo, co, src, target):
        span = pl.ds(pl.multiple_of((2 * zo + co) * shard, shard), shard)
        return pltpu.make_async_remote_copy(
            src_ref=src if src is not None else wfull.at[:, span, :],
            dst_ref=wfull.at[:, span, :],
            send_sem=wsend.at[n], recv_sem=wrecv.at[n],
            device_id={"seq": target})

    for dz in range(1, depth_z):
        w_copy(dz, z, core, w, z_peer(dz)).start()
    w_copy(depth_z, z, core, w, sibling).start()

    def t_copy(i, c):
        cols = pl.ds(0, width) if c is None else pl.ds(c * chunk, chunk)
        return pltpu.make_async_remote_copy(
            src_ref=send.at[i, pl.ds(0, sent), cols],
            dst_ref=recv.at[i, pl.ds(0, sent), cols],
            send_sem=tsend.at[i, 0 if c is None else c],
            recv_sem=trecv.at[i, 0 if c is None else c],
            device_id={"exp": there(i)})

    for c in range(chunks):
        x_copy(c).wait()
        for g in range(groups):
            got = jnp.dot(oh[g * GROUP * padded:(g + 1) * GROUP * padded, :], xbuf[c % 2],
                          preferred_element_type=f32).astype(bf16)
            got = got.reshape(GROUP, padded, chunk)
            cols = slice(c * chunk, (c + 1) * chunk)
            if g < groups - 1:
                send[g * GROUP:(g + 1) * GROUP, :, cols] = got
            else:
                send[g * GROUP:g * GROUP + GROUP - 1, :, cols] = got[:GROUP - 1]
                recv[peers - 1, :, cols] = got[GROUP - 1]
            if g == 0:
                for i in range(GROUP):
                    t_copy(i, c).start()
            elif c == chunks - 1:
                for i in range(g * GROUP, min((g + 1) * GROUP, peers - 1)):
                    t_copy(i, None).start()
        if c + 2 < chunks:
            x_copy(c + 2).start()

    local_w.wait()
    for dz in [d for d in (1, 3, 2) if d < depth_z]:
        zo = lax.rem(z - dz + depth_z, depth_z)
        w_copy(dz, zo, core, None, seq).wait_recv()
        w_copy(depth_z + dz, zo, core, None, sibling).start()
    for dz in range(depth_z):
        zo = lax.rem(z - dz + depth_z, depth_z)
        w_copy(depth_z + dz, zo, 1 - core, None, sibling).wait_recv()

    def r_copy(i):
        return pltpu.make_async_remote_copy(
            src_ref=send.at[i, pl.ds(0, sent), pl.ds(0, hidden)],
            dst_ref=rr.at[i, pl.ds(0, sent), :],
            send_sem=rsend.at[i], recv_sem=rrecv.at[i],
            device_id={"exp": back(i)})

    def members(g):
        return range(g * GROUP, min((g + 1) * GROUP, peers - 1))

    step = min(256, hidden)
    for g in range(groups):
        for i in members(g):
            for c in range(chunks if g == 0 else 1):
                copy = t_copy(i, c if g == 0 else None)
                copy.wait_send()
                copy.wait_recv()

        def product(n, carry, g=g):
            cols = pl.ds(pl.multiple_of(n * step, step), step)
            left = recv[g * GROUP:(g + 1) * GROUP].reshape(GROUP * padded, width)
            first = jnp.dot(left, wfull[0, :, cols], preferred_element_type=f32)
            second = jnp.dot(left, wfull[1, :, cols], preferred_element_type=f32)
            first = first.reshape(GROUP, padded, step)
            second = second.reshape(GROUP, padded, step)
            r = lax.broadcasted_iota(jnp.int32, (GROUP, padded, step), 1)
            both = jnp.where(r < cap, first, second).astype(bf16)
            if g < groups - 1:
                send[g * GROUP:(g + 1) * GROUP, :, cols] = both
            else:
                send[g * GROUP:g * GROUP + GROUP - 1, :, cols] = both[:GROUP - 1]
                rr[peers - 1, :, cols] = both[GROUP - 1]
            return carry

        lax.fori_loop(0, hidden // step, product, 0)
        for i in members(g):
            r_copy(i).start()

    ra, rb = routes[:, 0:1], routes[:, 1:2]
    lanes = max(experts, 128)
    names = lax.broadcasted_iota(jnp.int32, (count, lanes), 1)
    hit_a, hit_b = names == ra, names == rb
    both = jnp.where(hit_a | hit_b, 1.0, 0.0).astype(bf16)
    earlier = jnp.where(
        lax.broadcasted_iota(jnp.int32, (count, count), 1)
        < lax.broadcasted_iota(jnp.int32, (count, count), 0), 1.0, 0.0).astype(bf16)
    table = (jnp.dot(earlier, both, preferred_element_type=f32)
             + (names * cap).astype(f32))
    pos_a = jnp.sum(jnp.where(hit_a, table, 0.0), axis=1, keepdims=True)
    pos_b = jnp.sum(jnp.where(hit_b, table, 0.0), axis=1, keepdims=True)
    gate_a, gate_b = gates[:, 0:1], gates[:, 1:2]

    for g in range(groups):
        lane = lax.broadcasted_iota(jnp.int32, (1, GROUP * padded), 1)
        target = jnp.full_like(lane, -1)
        for j in range(GROUP):
            r = lane - j * padded
            target = jnp.where((r >= 0) & (r < rows), r + rows * there(g * GROUP + j), target)
        target = target.astype(f32)
        mix = jnp.where(pos_a == target, gate_a, 0.0) + jnp.where(pos_b == target, gate_b, 0.0)
        high = mix.astype(bf16)
        low = (mix - high.astype(f32)).astype(bf16)
        for i in members(g):
            r_copy(i).wait_recv()
        right = rr[g * GROUP:(g + 1) * GROUP]
        r = lax.broadcasted_iota(jnp.int32, right.shape, 1)
        right = jnp.where(r < rows, right, jnp.zeros_like(right))
        right = right.reshape(GROUP * padded, hidden)
        part = (jnp.dot(high, right, preferred_element_type=f32)
                + jnp.dot(low, right, preferred_element_type=f32))
        if g == 0:
            acc[...] = part
        elif g < groups - 1:
            acc[...] += part
        else:
            out[...] = (acc[...] + part).astype(bf16)

    for i in range(peers - 1):
        r_copy(i).wait_send()
    for dz in range(1, depth_z):
        w_copy(dz, z, core, w, z_peer(dz)).wait_send()
    w_copy(depth_z, z, core, w, sibling).wait_send()
    for dz in range(1, depth_z):
        zo = lax.rem(z - dz + depth_z, depth_z)
        w_copy(depth_z + dz, zo, core, None, sibling).wait_send()


def body(side, depth_z, tokens, routes, gates, weights):
    peers = side * side
    count, width = tokens.shape
    hidden = weights.shape[2]
    cap = 5 * count // (4 * peers)
    rows = 2 * cap
    padded = -(-rows // 16) * 16
    bf16 = jnp.bfloat16
    dma = pltpu.SemaphoreType.DMA
    vmem = pl.BlockSpec(memory_space=pltpu.VMEM)
    anywhere = pl.BlockSpec(memory_space=pl.ANY)
    return pl.pallas_call(
        functools.partial(kernel, side, depth_z, cap),
        out_shape=jax.ShapeDtypeStruct((count, hidden), bf16),
        in_specs=[anywhere, vmem, vmem, vmem, anywhere],
        out_specs=vmem,
        scratch_shapes=[
            pltpu.VMEM((peers - 1, padded, width), bf16),
            pltpu.VMEM((peers, padded, width), bf16),
            pltpu.VMEM((2, width, hidden), bf16),
            pltpu.VMEM((peers, padded, hidden), bf16),
            pltpu.VMEM((peers * padded, count), bf16),
            pltpu.VMEM((2, count, width // 4), bf16),
            pltpu.VMEM((count, hidden), jnp.float32),
            dma((2,)),
            dma((peers, 4)),
            dma((peers, 4)),
            dma((peers,)),
            dma((peers,)),
            dma,
            dma((2 * depth_z,)),
            dma((2 * depth_z,)),
        ],
        compiler_params=pltpu.CompilerParams(
            collective_id=0, has_side_effects=True, vmem_limit_bytes=67043328),
    )(tokens, routes, routes.T, gates, weights)


def solution(mesh):
    side = {4: 2, 16: 4}[mesh.shape["exp"]]
    return jax.shard_map(
        functools.partial(body, side, mesh.shape["seq"] // 2),
        mesh=mesh,
        in_specs=(
            P(("seq", "exp"), None),
            P(("seq", "exp"), None),
            P(("seq", "exp"), None),
            P("exp", "seq", None),
        ),
        out_specs=P(("seq", "exp"), None),
        check_vma=False,
    )
```

time: 393 us -> 242 us (0.62)
  Pallas kernels: 0 us -> 236 us
  blocking collectives: 151 us -> 0 us
  local copies, waits for them, and re-layouts: 101 us -> 5.67 us
  matrix products: 53.3 us -> 0 us
  waiting for transfers between devices: 45.2 us -> 0 us
  other arithmetic: 20.4 us -> 0 us
  between operations: 13.5 us -> 0.01 us
  starting transfers between devices: 5.99 us -> 0 us
    pallas_call x0 -> x1, Pallas kernels: none -> 236 us  [body(): pl.pallas_call(functools.partial(kernel, side, depth_z, cap), out_shape=j...]
    all_to_all x1 -> x0, blocking collectives: 151 us -> none  [body(): lax.all_to_all(outgoing, 'exp', split_axis=0, concat_axis=0, tiled=True)]
    dot_general x1 -> x0, matrix products: 53.3 us -> none  [body(): jnp.einsum('sjcd,jdf->sjcf', lax.all_to_all(outgoing, 'exp', split_axis=0...]
    all_to_all x1 -> x0, waiting for transfers between devices: 44.5 us -> none  [body(): lax.all_to_all(jnp.einsum('sjcd,jdf->sjcf', lax.all_to_all(outgoing, 'exp...]
    reshape x3 -> x0, local copies, waits for them, and re-layouts: 35.9 us -> none  [the longest x2 32.7 us: body(): outgoing = padded[slot_rows].reshape(groups, per_group, capacity, width)]
    gather x2 -> x0, local copies, waits for them, and re-layouts: 33.2 us -> none  [the longest x1 28.1 us: body(): outgoing = padded[slot_rows].reshape(groups, per_group, capacity, width)]
    convert_element_type x2 -> x0, local copies, waits for them, and re-layouts: 13.9 us -> none  [the longest x1 7.11 us: body(): returned = lax.all_to_all(jnp.einsum('sjcd,jdf->sjcf', lax.all_to_all(out...]
    reduce_sum x2 -> x0, other arithmetic: 10.4 us -> none  [the longest x1 10.3 us: body(): mixed = jnp.sum(picked * gates[:, :, None], axis=1)]
  transfers between devices with their start and end apart: 2 -> 0, of which waited for: 1 -> 0; matrix products, arithmetic and copies ran while one was open for 22% -> 0% of each run, Pallas kernels for 0% -> 0%
where the time goes in v1:
time: 242 us
  Pallas kernels  236 us (98%)
  local copies, waits for them, and re-layouts  5.67 us (2%)
    pallas_call x1, Pallas kernels, body(): pl.pallas_call(functools.partial(kernel, side, depth_z, cap), out_shape=j...  236 us
    unnamed x3, local copies, waits for them, and re-layouts  5.67 us

profile of v1, /device:TPU:24, one launch (start us, length us, event | category | flops | bytes accessed | tf_op | source)
XLA Modules:
  0.0 241.6 jit_solution(12724932612088890992)
XLA Ops:
  0.0 1.6 copy.6.gates
  1.6 1.6 copy.5.routes
  3.2 235.9 %shard_map.46 = bf16[640,1024]{1,0:T(8,128)(2,1)} custom-call(bf16[640,4096]{1,0:T(8,128)(2,1)} %tok.1, s32[640,2]{1,0:T(8,128)} %copy.5.routes, s32[2,640]{1,0:T(2,128)} %bitcast.1, f32[640,2]{1,0:T(8,128)} %copy.6.gates, bf16[2,512,1024]{2,1,0:T(8,128)(2,1)} %w.1), custom_call_target="tpu_custom_call" | custom-call | tf_op jit(solution)/shard_map/pallas_call | solution.py:246
  239.1 2.5 %copy.8 = bf16[640,1024]{1,0:T(8,128)(2,1)} copy(bf16[640,1024]{1,0:T(8,128)(2,1)} %shard_map.46) | data formatting | bytes 2621440

commit v2 on v0

v2 whole, which is shorter than its diff:
```python
import functools

import jax
import jax.numpy as jnp
from jax import lax
from jax.experimental import pallas as pl
from jax.experimental.pallas import tpu as pltpu
from jax.sharding import PartitionSpec as P

SIDE = 4
DEPTH = 4
GROUP = 4
TILE = 8
SENDS = [("b", 2), ("d", 2), ("b", 1), ("d", 1), ("b", 3), ("d", 3), ("b", 0), ("d", 0),
         ("a", 2), ("c", 2), ("a", 1), ("c", 1), ("a", 3), ("c", 3), ("a", 0), ("c", 0)]
SLOTS = [("a", 0), ("b", 0), ("a", 2), ("a", 1), ("a", 3), ("b", 2), ("b", 1), ("b", 3),
         ("c", 0), ("d", 0), ("c", 2), ("c", 1), ("c", 3), ("d", 2), ("d", 1), ("d", 3)]
SELF = [("a", 0), ("c", 0)]
RELAYED = [("b", 2), ("d", 2), ("b", 1), ("d", 1), ("b", 3), ("d", 3)]


def flip(v):
    return v + 1 - 2 * lax.rem(v, 2)


def choose(v, parity, even, odd):
    return even + (odd - even) * lax.rem(parity, 2)


def mate(v, parity):
    return choose(v, parity, flip(v), SIDE - 1 - v)


def beside(v, parity):
    return choose(v, parity, SIDE - 1 - v, flip(v))


def kernel(cap, tok, routes, routes_t, gates, w, out, held,
           send, recv, land, res, rr_lo, rr_hi, oh, xbuf, wbuf, acc, pos,
           xsem, wbsem, tsend, trecv, usend, urecv, lsend, lrecv, hsend, hrecv,
           wloc, wsend, wrecv):
    count, width = tok.shape
    shard, hidden = w.shape[1:]
    rows = 2 * cap
    padded = recv.shape[1]
    sent = -(-rows // TILE) * TILE
    low_rows = cap // 16 * 16
    span = padded - low_rows
    peers = SIDE * SIDE
    experts = 2 * peers
    chunks = 4
    chunk = width // chunks
    f32, bf16 = jnp.float32, jnp.bfloat16

    seq = lax.axis_index("seq")
    exp = lax.axis_index("exp")
    z, core = seq // 2, lax.rem(seq, 2)
    y, x = exp // SIDE, lax.rem(exp, SIDE)
    sibling = 2 * z + 1 - core

    def turn(v, d):
        return lax.rem(v + d + SIDE, SIDE)

    def place(yy, xx):
        return yy * SIDE + xx

    def goal(m):
        kind, d = m
        if kind == "a":
            yy, xx = turn(y, d), x
        elif kind == "b":
            yy = turn(y, d)
            xx = beside(x, yy)
        elif kind == "c":
            yy, xx = y, turn(x, d)
        else:
            xx = turn(x, d)
            yy = beside(y, xx)
        if kind in "ab":
            return (yy, xx), (yy, mate(xx, yy)), 0
        return (yy, xx), (mate(yy, xx), xx), 1

    def corner(m):
        kind, d = m
        if kind == "b":
            return place(y, beside(x, turn(y, d)))
        if kind == "d":
            return place(beside(y, turn(x, d)), x)
        return place(*goal(m)[0])

    def origin(m):
        kind, d = m
        if kind == "a":
            return place(turn(y, -d), x)
        if kind == "b":
            return place(turn(y, -d), beside(x, y))
        if kind == "c":
            return place(y, turn(x, -d))
        return place(beside(y, x), turn(x, -d))

    def names_of(m):
        first, second, which = goal(m)
        return 2 * place(*first) + which, 2 * place(*second) + which

    def rows_of(zz, cc):
        return pl.ds(pl.multiple_of((2 * zz + cc) * shard, shard), shard)

    local_w = pltpu.make_async_copy(w, held.at[pl.ds(0, 2), rows_of(z, core), :], wloc)
    local_w.start()

    def x_copy(c):
        return pltpu.make_async_copy(
            tok.at[:, pl.ds(c * chunk, chunk)], xbuf.at[c % 2], xsem.at[c % 2])

    x_copy(0).start()
    x_copy(1).start()

    barrier = pltpu.get_barrier_semaphore()
    for i in range(1, peers):
        pl.semaphore_signal(barrier, inc=1, device_id={"exp": lax.rem(exp + i, peers)})
    up, down = 2 * lax.rem(z + 1, DEPTH) + core, 2 * lax.rem(z + DEPTH - 1, DEPTH) + core
    for other in (up, down, sibling):
        pl.semaphore_signal(barrier, inc=1, device_id={"seq": other})

    ra, rb = routes_t[0:1, :], routes_t[1:2, :]
    names = lax.broadcasted_iota(jnp.int32, (experts, count), 0)
    hit_a, hit_b = names == ra, names == rb
    both = jnp.where(hit_a | hit_b, 1.0, 0.0).astype(bf16)
    earlier = jnp.where(
        lax.broadcasted_iota(jnp.int32, (count, count), 0)
        < lax.broadcasted_iota(jnp.int32, (count, count), 1), 1.0, 0.0).astype(bf16)
    table = (jnp.dot(both, earlier, preferred_element_type=f32)
             + (names * cap).astype(f32))
    pos_a = jnp.sum(jnp.where(hit_a, table, 0.0), axis=0, keepdims=True)
    pos_b = jnp.sum(jnp.where(hit_b, table, 0.0), axis=0, keepdims=True)

    for i, m in enumerate(SENDS):
        e1, e2 = names_of(m)
        r = lax.broadcasted_iota(jnp.int32, (padded, count), 0)
        target = jnp.where(r < cap, r + e1 * cap, r - cap + e2 * cap)
        target = jnp.where(r < rows, target, -1).astype(f32)
        hit = (pos_a == target) | (pos_b == target)
        oh[i * padded:(i + 1) * padded, :] = jnp.where(hit, 1.0, 0.0).astype(bf16)

    pl.semaphore_wait(barrier, peers - 1 + 3)

    prev, after, far = turn(z, -1), turn(z, 1), turn(z, 2)

    def w_copy(n, part, zz, cc, expert, many, target, mine=False):
        dst = held.at[pl.ds(expert, many), rows_of(zz, cc), :]
        return pltpu.make_async_remote_copy(
            src_ref=w if mine else dst, dst_ref=dst,
            send_sem=wsend.at[10 * part + n], recv_sem=wrecv.at[10 * part + n],
            device_id={"seq": target})

    def swap(j):
        target = place(y, mate(x, y)) if j == 0 else place(mate(y, x), x)
        return pltpu.make_async_remote_copy(
            src_ref=w.at[pl.ds(j, 1)], dst_ref=held.at[pl.ds(2 + j, 1), rows_of(z, core), :],
            send_sem=wsend.at[20 + j], recv_sem=wrecv.at[20 + j], device_id={"exp": target})

    def w_up(p):
        return w_copy(0, p, z, core, 2 * p, 2, up, mine=p == 0)

    def w_down(p):
        return w_copy(1, p, z, core, 2 * p, 2, down, mine=p == 0)

    def w_up_far(p):
        return w_copy(2, p, prev, core, 2 * p, 1, up)

    def w_down_far(p):
        return w_copy(3, p, after, core, 2 * p + 1, 1, down)

    def w_side(p, n, cc):
        zz, expert, many = [(z, 2 * p, 2), (prev, 2 * p, 2), (after, 2 * p, 2),
                            (far, 2 * p, 1), (far, 2 * p + 1, 1)][n]
        return w_copy(4 + n, p, zz, cc, expert, many, sibling, mine=(p == 0 and n == 0 and cc is core))

    def got(copy_n, p):
        zz, expert, many = [(prev, 2 * p, 2), (after, 2 * p, 2), (far, 2 * p, 1), (far, 2 * p + 1, 1)][copy_n]
        w_copy(copy_n, p, zz, core, expert, many, up).wait_recv()

    w_up(0).start()
    w_down(0).start()
    swap(0).start()
    swap(1).start()
    w_side(0, 0, core).start()

    def t_copy(m, c):
        i = SENDS.index(m)
        cols = pl.ds(0, width) if c is None else pl.ds(c * chunk, chunk)
        if m in RELAYED:
            dst = land.at[RELAYED.index(m), pl.ds(0, sent), cols]
        else:
            dst = recv.at[SLOTS.index(m), pl.ds(0, sent), cols]
        k = 0 if c is None else c
        return pltpu.make_async_remote_copy(
            src_ref=send.at[i, pl.ds(0, sent), cols], dst_ref=dst,
            send_sem=tsend.at[i, k], recv_sem=trecv.at[i, k], device_id={"exp": corner(m)})

    def pieces(m):
        return range(chunks) if SENDS.index(m) < GROUP else [None]

    def u_copy(m):
        kind, d = m
        target = place(turn(y, d), x) if kind == "b" else place(y, turn(x, d))
        i = RELAYED.index(m)
        return pltpu.make_async_remote_copy(
            src_ref=land.at[i, pl.ds(0, sent), :],
            dst_ref=recv.at[SLOTS.index(m), pl.ds(0, sent), :],
            send_sem=usend.at[i], recv_sem=urecv.at[i], device_id={"exp": target})

    groups = peers // GROUP
    for c in range(chunks):
        x_copy(c).wait()
        cols = slice(c * chunk, (c + 1) * chunk)
        for g in range(groups):
            got_rows = jnp.dot(oh[g * GROUP * padded:(g + 1) * GROUP * padded, :], xbuf[c % 2],
                               preferred_element_type=f32).astype(bf16)
            got_rows = got_rows.reshape(GROUP, padded, chunk)
            ms = SENDS[g * GROUP:(g + 1) * GROUP]
            if g < groups - 1:
                send[g * GROUP:(g + 1) * GROUP, :, cols] = got_rows
            else:
                for j, m in enumerate(ms):
                    if m in SELF:
                        recv[SLOTS.index(m), :, cols] = got_rows[j]
                    else:
                        send[g * GROUP + j, :, cols] = got_rows[j]
            for m in ms:
                if m in SELF:
                    continue
                if g == 0:
                    t_copy(m, c).start()
                elif c == chunks - 1:
                    t_copy(m, None).start()
        if c + 2 < chunks:
            x_copy(c + 2).start()

    def landed(m):
        for c in pieces(m):
            t_copy(m, c).wait_recv()

    def relay(m):
        landed(m)
        u_copy(m).start()

    for m in RELAYED[:4]:
        relay(m)

    local_w.wait()
    got(0, 0)
    w_up_far(0).start()
    got(1, 0)
    w_down_far(0).start()
    swap(0).wait_recv()
    swap(1).wait_recv()
    w_up(1).start()
    w_down(1).start()
    w_side(0, 1, core).start()
    w_side(0, 2, core).start()
    w_side(1, 0, core).start()
    for m in RELAYED[4:]:
        relay(m)

    ra, rb = routes[:, 0:1], routes[:, 1:2]
    lanes = max(experts, 128)
    names = lax.broadcasted_iota(jnp.int32, (count, lanes), 1)
    hit_a, hit_b = names == ra, names == rb
    both = jnp.where(hit_a | hit_b, 1.0, 0.0).astype(bf16)
    earlier = jnp.where(
        lax.broadcasted_iota(jnp.int32, (count, count), 1)
        < lax.broadcasted_iota(jnp.int32, (count, count), 0), 1.0, 0.0).astype(bf16)
    table = (jnp.dot(earlier, both, preferred_element_type=f32)
             + (names * cap).astype(f32))
    pos[:, 0:1] = jnp.sum(jnp.where(hit_a, table, 0.0), axis=1, keepdims=True)
    pos[:, 1:2] = jnp.sum(jnp.where(hit_b, table, 0.0), axis=1, keepdims=True)

    got(2, 0)
    w_side(0, 3, core).start()
    got(3, 0)
    w_side(0, 4, core).start()
    for n in range(5):
        w_side(0, n, 1 - core).wait_recv()

    step = wbuf.shape[2]

    def w_load(q, n, slot):
        cols = pl.ds(pl.multiple_of(n * step, step), step)
        return pltpu.make_async_copy(held.at[q, :, cols], wbuf.at[slot], wbsem.at[slot])

    def product(base, q, half):
        start = 0 if half == 0 else low_rows
        w_load(q, 0, 0).start()

        def one(n, carry):
            slot = lax.rem(n, 2)
            w_load(q, n, slot).wait()

            @pl.when(n + 1 < hidden // step)
            def _():
                w_load(q, n + 1, 1 - slot).start()

            cols = pl.ds(pl.multiple_of(n * step, step), step)
            left = recv[base:base + GROUP, start:start + span, :].reshape(GROUP * span, width)
            prod = jnp.dot(left, wbuf[slot], preferred_element_type=f32).astype(bf16)
            prod = prod.reshape(GROUP, span, step)
            if half == 0:
                res[base:base + GROUP, 0:span, cols] = prod
            else:
                edge = res[base:base + GROUP, low_rows:low_rows + 16, cols]
                r = lax.broadcasted_iota(jnp.int32, edge.shape, 1)
                res[base:base + GROUP, low_rows:low_rows + 16, cols] = jnp.where(
                    r < cap - low_rows, edge, prod[:, 0:16])
                res[base:base + GROUP, low_rows + 16:padded, cols] = prod[:, 16:]
            return carry

        lax.fori_loop(0, hidden // step, one, 0)

    def low_copy(m):
        i = SLOTS.index(m)
        return pltpu.make_async_remote_copy(
            src_ref=res.at[i, pl.ds(0, low_rows), :], dst_ref=rr_lo.at[i],
            send_sem=lsend.at[i], recv_sem=lrecv.at[i], device_id={"exp": origin(m)})

    def high_copy(m):
        i = SLOTS.index(m)
        return pltpu.make_async_remote_copy(
            src_ref=res.at[i, pl.ds(low_rows, sent - low_rows), :],
            dst_ref=rr_hi.at[i, pl.ds(0, sent - low_rows), :],
            send_sem=hsend.at[i], recv_sem=hrecv.at[i], device_id={"exp": origin(m)})

    def arrived(m):
        if m in SELF:
            return
        if m in RELAYED:
            u_copy(m).wait_recv()
        else:
            landed(m)

    def give_low(base):
        for i in range(base, base + GROUP):
            if SLOTS[i] in SELF:
                rr_lo[i] = res[i, 0:low_rows, :]
            else:
                low_copy(SLOTS[i]).start()

    def give_high(base):
        for i in range(base, base + GROUP):
            if SLOTS[i] in SELF:
                rr_hi[i] = res[i, low_rows:padded, :]
            else:
                high_copy(SLOTS[i]).start()

    for base, q in ((0, 0), (8, 1)):
        for m in SLOTS[base:base + GROUP]:
            arrived(m)
        product(base, q, 0)
        give_low(base)

    got(0, 1)
    w_up_far(1).start()
    got(1, 1)
    w_down_far(1).start()
    w_side(1, 1, core).start()
    w_side(1, 2, core).start()

    for base, q in ((4, 0), (12, 1)):
        for m in SLOTS[base:base + GROUP]:
            arrived(m)
        product(base, q, 0)
        give_low(base)

    got(2, 1)
    w_side(1, 3, core).start()
    got(3, 1)
    w_side(1, 4, core).start()
    for n in range(5):
        w_side(1, n, 1 - core).wait_recv()

    for base, q in ((0, 2), (8, 3), (4, 2), (12, 3)):
        product(base, q, 1)
        give_high(base)

    gate_a, gate_b = gates[:, 0:1], gates[:, 1:2]
    pos_a, pos_b = pos[:, 0:1], pos[:, 1:2]

    def mixed(base, high):
        size = span if high else low_rows
        lane = lax.broadcasted_iota(jnp.int32, (1, GROUP * size), 1)
        target = jnp.full_like(lane, -1)
        for j in range(GROUP):
            e1, e2 = names_of(SLOTS[base + j])
            local = lane - j * size
            r = local + (low_rows if high else 0)
            value = jnp.where(r < cap, r + e1 * cap, r - cap + e2 * cap)
            target = jnp.where((local >= 0) & (local < size) & (r < rows), value, target)
        target = target.astype(f32)
        mix = jnp.where(pos_a == target, gate_a, 0.0) + jnp.where(pos_b == target, gate_b, 0.0)
        top = mix.astype(bf16)
        rest = (mix - top.astype(f32)).astype(bf16)
        for m in SLOTS[base:base + GROUP]:
            if m not in SELF:
                (high_copy(m) if high else low_copy(m)).wait_recv()
        if high:
            right = rr_hi[base:base + GROUP]
            r = lax.broadcasted_iota(jnp.int32, right.shape, 1)
            right = jnp.where(r < rows - low_rows, right, jnp.zeros_like(right))
        else:
            right = rr_lo[base:base + GROUP]
        right = right.reshape(GROUP * size, hidden)
        return (jnp.dot(top, right, preferred_element_type=f32)
                + jnp.dot(rest, right, preferred_element_type=f32))

    order = [(0, False), (8, False), (4, False), (12, False),
             (0, True), (8, True), (4, True), (12, True)]
    for k, (base, high) in enumerate(order):
        part = mixed(base, high)
        if k == 0:
            acc[...] = part
        elif k < len(order) - 1:
            acc[...] += part
        else:
            out[...] = (acc[...] + part).astype(bf16)

    for m in SENDS:
        if m not in SELF:
            for c in pieces(m):
                t_copy(m, c).wait_send()
            low_copy(m).wait_send()
            high_copy(m).wait_send()
    for m in RELAYED:
        u_copy(m).wait_send()
    swap(0).wait_send()
    swap(1).wait_send()
    for p in range(2):
        for copy in (w_up(p), w_down(p), w_up_far(p), w_down_far(p)):
            copy.wait_send()
        for n in range(5):
            w_side(p, n, core).wait_send()


def body(tokens, routes, gates, weights):
    peers = SIDE * SIDE
    count, width = tokens.shape
    shard, hidden = weights.shape[1:]
    cap = 5 * count // (4 * peers)
    rows = 2 * cap
    padded = -(-rows // 16) * 16
    low_rows = cap // 16 * 16
    span = padded - low_rows
    bf16 = jnp.bfloat16
    dma = pltpu.SemaphoreType.DMA
    vmem = pl.BlockSpec(memory_space=pltpu.VMEM)
    anywhere = pl.BlockSpec(memory_space=pl.ANY)
    step = min(256, hidden)
    mixed, _ = pl.pallas_call(
        functools.partial(kernel, cap),
        out_shape=(
            jax.ShapeDtypeStruct((count, hidden), bf16),
            jax.ShapeDtypeStruct((4, width, hidden), bf16),
        ),
        in_specs=[anywhere, vmem, vmem, vmem, anywhere],
        out_specs=(vmem, anywhere),
        scratch_shapes=[
            pltpu.VMEM((peers - 2, padded, width), bf16),
            pltpu.VMEM((peers, padded, width), bf16),
            pltpu.VMEM((len(RELAYED), padded, width), bf16),
            pltpu.VMEM((peers, padded, hidden), bf16),
            pltpu.VMEM((peers, low_rows, hidden), bf16),
            pltpu.VMEM((peers, span, hidden), bf16),
            pltpu.VMEM((peers * padded, count), bf16),
            pltpu.VMEM((2, count, width // 4), bf16),
            pltpu.VMEM((2, width, step), bf16),
            pltpu.VMEM((count, hidden), jnp.float32),
            pltpu.VMEM((count, 128), jnp.float32),
            dma((2,)),
            dma((2,)),
            dma((peers, 4)),
            dma((peers, 4)),
            dma((len(RELAYED),)),
            dma((len(RELAYED),)),
            dma((peers,)),
            dma((peers,)),
            dma((peers,)),
            dma((peers,)),
            dma,
            dma((22,)),
            dma((22,)),
        ],
        compiler_params=pltpu.CompilerParams(
            collective_id=0, has_side_effects=True, vmem_limit_bytes=67043328),
    )(tokens, routes, routes.T, gates, weights)
    return mixed


def solution(mesh):
    if mesh.shape["exp"] != SIDE * SIDE or mesh.shape["seq"] != 2 * DEPTH:
        raise ValueError("mesh")
    return jax.shard_map(
        body,
        mesh=mesh,
        in_specs=(
            P(("seq", "exp"), None),
            P(("seq", "exp"), None),
            P(("seq", "exp"), None),
            P("exp", "seq", None),
        ),
        out_specs=P(("seq", "exp"), None),
        check_vma=False,
    )
```

time: 393 us -> 218 us (0.55)
  Pallas kernels: 0 us -> 208 us
  blocking collectives: 151 us -> 0 us
  local copies, waits for them, and re-layouts: 101 us -> 5.66 us
  matrix products: 53.3 us -> 0 us
  waiting for transfers between devices: 45.2 us -> 0 us
  other arithmetic: 20.4 us -> 0 us
  between operations: 13.5 us -> 0.01 us
  starting transfers between devices: 5.99 us -> 0 us
    pallas_call x0 -> x1, Pallas kernels: none -> 208 us  [body(): pl.pallas_call(functools.partial(kernel, cap), out_shape=(jax.ShapeDtypeS...]
    all_to_all x1 -> x0, blocking collectives: 151 us -> none  [body(): lax.all_to_all(outgoing, 'exp', split_axis=0, concat_axis=0, tiled=True)]
    dot_general x1 -> x0, matrix products: 53.3 us -> none  [body(): jnp.einsum('sjcd,jdf->sjcf', lax.all_to_all(outgoing, 'exp', split_axis=0...]
    all_to_all x1 -> x0, waiting for transfers between devices: 44.5 us -> none  [body(): lax.all_to_all(jnp.einsum('sjcd,jdf->sjcf', lax.all_to_all(outgoing, 'exp...]
    reshape x3 -> x0, local copies, waits for them, and re-layouts: 35.9 us -> none  [the longest x2 32.7 us: body(): outgoing = padded[slot_rows].reshape(groups, per_group, capacity, width)]
    gather x2 -> x0, local copies, waits for them, and re-layouts: 33.2 us -> none  [the longest x1 28.1 us: body(): outgoing = padded[slot_rows].reshape(groups, per_group, capacity, width)]
    convert_element_type x2 -> x0, local copies, waits for them, and re-layouts: 13.9 us -> none  [the longest x1 7.11 us: body(): returned = lax.all_to_all(jnp.einsum('sjcd,jdf->sjcf', lax.all_to_all(out...]
    reduce_sum x2 -> x0, other arithmetic: 10.4 us -> none  [the longest x1 10.3 us: body(): mixed = jnp.sum(picked * gates[:, :, None], axis=1)]
  transfers between devices with their start and end apart: 2 -> 0, of which waited for: 1 -> 0; matrix products, arithmetic and copies ran while one was open for 22% -> 0% of each run, Pallas kernels for 0% -> 0%
where the time goes in v2:
time: 218 us; the launch traced here: 214 us
  Pallas kernels  208 us (95%)
  local copies, waits for them, and re-layouts  5.66 us (3%)
    pallas_call x1, Pallas kernels, body(): pl.pallas_call(functools.partial(kernel, cap), out_shape=(jax.ShapeDtypeS...  208 us
    unnamed x3, local copies, waits for them, and re-layouts  5.66 us

profile of v2, /device:TPU:24, one launch (start us, length us, event | category | flops | bytes accessed | tf_op | source)
XLA Modules:
  0.0 213.9 jit_solution(5150002715531416161)
XLA Ops:
  0.0 1.6 copy.6.gates
  1.6 1.6 copy.5.routes
  3.2 208.2 %shard_map.46 = (bf16[640,1024]{1,0:T(8,128)(2,1)}, bf16[4,4096,1024]{2,1,0:T(8,128)(2,1)}) custom-call(bf16[640,4096]{1,0:T(8,128)(2,1)} %tok.1, s32[640,2]{1,0:T(8,128)} %copy.5.routes, s32[2,640]{1,0:T(2,128)} %bitcast.1, f32[640,2]{1,0:T(8,128)} %copy.6.gates, bf16[2,512,1024]{2,1,0:T(8,128)(2,1)} %w.1), custom_call_target="tpu_custom_call" | custom-call | tf_op jit(solution)/shard_map/pallas_call | solution.py:457
  211.4 2.5 %copy.8 = bf16[640,1024]{1,0:T(8,128)(2,1)} copy(bf16[640,1024]{1,0:T(8,128)(2,1)} %get-tuple-element.6) | data formatting | bytes 2621440

commit v3 on v2

v3 whole, which is shorter than its diff:
```python
import functools

import jax
import jax.numpy as jnp
from jax import lax
from jax.experimental import pallas as pl
from jax.experimental.pallas import tpu as pltpu
from jax.sharding import PartitionSpec as P

SIDE = 4
DEPTH = 4
GROUP = 4
TILE = 8
SENDS = [("b", 2), ("d", 2), ("b", 1), ("d", 1), ("b", 3), ("d", 3), ("b", 0), ("d", 0),
         ("a", 2), ("c", 2), ("a", 1), ("c", 1), ("a", 3), ("c", 3), ("a", 0), ("c", 0)]
SLOTS = [("a", 0), ("b", 0), ("a", 2), ("a", 1), ("a", 3), ("b", 2), ("b", 1), ("b", 3),
         ("c", 0), ("d", 0), ("c", 2), ("c", 1), ("c", 3), ("d", 2), ("d", 1), ("d", 3)]
SELF = [("a", 0), ("c", 0)]
RELAYED = [("b", 2), ("d", 2), ("b", 1), ("d", 1), ("b", 3), ("d", 3)]


def flip(v):
    return v + 1 - 2 * lax.rem(v, 2)


def choose(v, parity, even, odd):
    return even + (odd - even) * lax.rem(parity, 2)


def mate(v, parity):
    return choose(v, parity, flip(v), SIDE - 1 - v)


def beside(v, parity):
    return choose(v, parity, SIDE - 1 - v, flip(v))


def kernel(cap, tok, routes, gates, w, out, held,
           recv, land, rr_lo, rr_hi,
           xsem, wosem, wbsem, tsend, trecv, usend, urecv, lsend, lrecv, hsend, hrecv,
           wloc, wsend, wrecv):
    count, width = tok.shape
    shard, hidden = w.shape[1:]
    rows = 2 * cap
    padded = recv.shape[1]
    sent = -(-rows // TILE) * TILE
    low_rows = cap // 16 * 16
    span = padded - low_rows
    peers = SIDE * SIDE
    experts = 2 * peers
    chunks = 4
    chunk = width // chunks
    f32, bf16 = jnp.float32, jnp.bfloat16

    seq = lax.axis_index("seq")
    exp = lax.axis_index("exp")
    z, core = seq // 2, lax.rem(seq, 2)
    y, x = exp // SIDE, lax.rem(exp, SIDE)
    sibling = 2 * z + 1 - core

    def turn(v, d):
        return lax.rem(v + d + SIDE, SIDE)

    def place(yy, xx):
        return yy * SIDE + xx

    def goal(m):
        kind, d = m
        if kind == "a":
            yy, xx = turn(y, d), x
        elif kind == "b":
            yy = turn(y, d)
            xx = beside(x, yy)
        elif kind == "c":
            yy, xx = y, turn(x, d)
        else:
            xx = turn(x, d)
            yy = beside(y, xx)
        if kind in "ab":
            return (yy, xx), (yy, mate(xx, yy)), 0
        return (yy, xx), (mate(yy, xx), xx), 1

    def corner(m):
        kind, d = m
        if kind == "b":
            return place(y, beside(x, turn(y, d)))
        if kind == "d":
            return place(beside(y, turn(x, d)), x)
        return place(*goal(m)[0])

    def origin(m):
        kind, d = m
        if kind == "a":
            return place(turn(y, -d), x)
        if kind == "b":
            return place(turn(y, -d), beside(x, y))
        if kind == "c":
            return place(y, turn(x, -d))
        return place(beside(y, x), turn(x, -d))

    def names_of(m):
        first, second, which = goal(m)
        return 2 * place(*first) + which, 2 * place(*second) + which

    def rows_of(zz, cc):
        return pl.ds(pl.multiple_of((2 * zz + cc) * shard, shard), shard)

    local_w = pltpu.make_async_copy(w, held.at[pl.ds(0, 2), rows_of(z, core), :], wloc)
    local_w.start()

    barrier = pltpu.get_barrier_semaphore()
    for i in range(1, peers):
        pl.semaphore_signal(barrier, inc=1, device_id={"exp": lax.rem(exp + i, peers)})
    up, down = 2 * lax.rem(z + 1, DEPTH) + core, 2 * lax.rem(z + DEPTH - 1, DEPTH) + core
    for other in (up, down, sibling):
        pl.semaphore_signal(barrier, inc=1, device_id={"seq": other})

    ra, rb = routes[0:1, :], routes[1:2, :]
    names = lax.broadcasted_iota(jnp.int32, (experts, count), 0)
    hit_a, hit_b = names == ra, names == rb
    both = jnp.where(hit_a | hit_b, 1.0, 0.0).astype(bf16)
    earlier = jnp.where(
        lax.broadcasted_iota(jnp.int32, (count, count), 0)
        < lax.broadcasted_iota(jnp.int32, (count, count), 1), 1.0, 0.0).astype(bf16)
    table = (jnp.dot(both, earlier, preferred_element_type=f32)
             + (names * cap).astype(f32))
    pos_a = jnp.sum(jnp.where(hit_a, table, 0.0), axis=0, keepdims=True)
    pos_b = jnp.sum(jnp.where(hit_b, table, 0.0), axis=0, keepdims=True)

    pl.semaphore_wait(barrier, peers - 1 + 3)

    prev, after, far = turn(z, -1), turn(z, 1), turn(z, 2)

    def w_copy(n, part, zz, cc, expert, many, target, mine=False):
        dst = held.at[pl.ds(expert, many), rows_of(zz, cc), :]
        return pltpu.make_async_remote_copy(
            src_ref=w if mine else dst, dst_ref=dst,
            send_sem=wsend.at[10 * part + n], recv_sem=wrecv.at[10 * part + n],
            device_id={"seq": target})

    def swap(j):
        target = place(y, mate(x, y)) if j == 0 else place(mate(y, x), x)
        return pltpu.make_async_remote_copy(
            src_ref=w.at[pl.ds(j, 1)], dst_ref=held.at[pl.ds(2 + j, 1), rows_of(z, core), :],
            send_sem=wsend.at[20 + j], recv_sem=wrecv.at[20 + j], device_id={"exp": target})

    def w_up(p):
        return w_copy(0, p, z, core, 2 * p, 2, up, mine=p == 0)

    def w_down(p):
        return w_copy(1, p, z, core, 2 * p, 2, down, mine=p == 0)

    def w_up_far(p):
        return w_copy(2, p, prev, core, 2 * p, 1, up)

    def w_down_far(p):
        return w_copy(3, p, after, core, 2 * p + 1, 1, down)

    def w_side(p, n, cc):
        zz, expert, many = [(z, 2 * p, 2), (prev, 2 * p, 2), (after, 2 * p, 2),
                            (far, 2 * p, 1), (far, 2 * p + 1, 1)][n]
        return w_copy(4 + n, p, zz, cc, expert, many, sibling, mine=(p == 0 and n == 0 and cc is core))

    def got(copy_n, p):
        zz, expert, many = [(prev, 2 * p, 2), (after, 2 * p, 2), (far, 2 * p, 1), (far, 2 * p + 1, 1)][copy_n]
        w_copy(copy_n, p, zz, core, expert, many, up).wait_recv()

    w_up(0).start()
    w_down(0).start()
    swap(0).start()
    swap(1).start()
    w_side(0, 0, core).start()

    def t_copy(send, m, c):
        i = SENDS.index(m)
        cols = pl.ds(0, width) if c is None else pl.ds(c * chunk, chunk)
        if m in RELAYED:
            dst = land.at[RELAYED.index(m), pl.ds(0, sent), cols]
        else:
            dst = recv.at[SLOTS.index(m), pl.ds(0, sent), cols]
        k = 0 if c is None else c
        return pltpu.make_async_remote_copy(
            src_ref=send.at[i, pl.ds(0, sent), cols], dst_ref=dst,
            send_sem=tsend.at[i, k], recv_sem=trecv.at[i, k], device_id={"exp": corner(m)})

    def pieces(m):
        return range(chunks) if SENDS.index(m) < GROUP else [None]

    def u_copy(m):
        kind, d = m
        target = place(turn(y, d), x) if kind == "b" else place(y, turn(x, d))
        i = RELAYED.index(m)
        return pltpu.make_async_remote_copy(
            src_ref=land.at[i, pl.ds(0, sent), :],
            dst_ref=recv.at[SLOTS.index(m), pl.ds(0, sent), :],
            send_sem=usend.at[i], recv_sem=urecv.at[i], device_id={"exp": target})

    def dispatch(send, xbuf, oh):
        def x_copy(c):
            return pltpu.make_async_copy(
                tok.at[:, pl.ds(c * chunk, chunk)], xbuf.at[c % 2], xsem.at[c % 2])

        x_copy(0).start()
        x_copy(1).start()

        def place_rows(g):
            for i in range(g * GROUP, (g + 1) * GROUP):
                e1, e2 = names_of(SENDS[i])
                r = lax.broadcasted_iota(jnp.int32, (padded, count), 0)
                target = jnp.where(r < cap, r + e1 * cap, r - cap + e2 * cap)
                target = jnp.where(r < rows, target, -1).astype(f32)
                hit = (pos_a == target) | (pos_b == target)
                oh[i * padded:(i + 1) * padded, :] = jnp.where(hit, 1.0, 0.0).astype(bf16)

        groups = peers // GROUP
        for c in range(chunks):
            x_copy(c).wait()
            cols = slice(c * chunk, (c + 1) * chunk)
            for g in range(groups):
                if c == 0:
                    place_rows(g)
                got_rows = jnp.dot(oh[g * GROUP * padded:(g + 1) * GROUP * padded, :], xbuf[c % 2],
                                   preferred_element_type=f32).astype(bf16)
                got_rows = got_rows.reshape(GROUP, padded, chunk)
                ms = SENDS[g * GROUP:(g + 1) * GROUP]
                if g < groups - 1:
                    send[g * GROUP:(g + 1) * GROUP, :, cols] = got_rows
                else:
                    for j, m in enumerate(ms):
                        if m in SELF:
                            recv[SLOTS.index(m), :, cols] = got_rows[j]
                        else:
                            send[g * GROUP + j, :, cols] = got_rows[j]
                for m in ms:
                    if m in SELF:
                        continue
                    if g == 0:
                        t_copy(send, m, c).start()
                    elif c == chunks - 1:
                        t_copy(send, m, None).start()
            if c + 2 < chunks:
                x_copy(c + 2).start()

        def landed(m):
            for c in pieces(m):
                t_copy(send, m, c).wait_recv()

        def relay(m):
            landed(m)
            u_copy(m).start()

        swap(0).wait_recv()
        swap(1).wait_recv()
        w_up(1).start()
        w_down(1).start()
        w_side(1, 0, core).start()
        for m in RELAYED[:4]:
            relay(m)
        local_w.wait()
        got(0, 0)
        w_up_far(0).start()
        w_side(0, 1, core).start()
        got(1, 0)
        w_down_far(0).start()
        w_side(0, 2, core).start()
        for m in RELAYED[4:]:
            relay(m)
        got(0, 1)
        w_up_far(1).start()
        w_side(1, 1, core).start()
        got(1, 1)
        w_down_far(1).start()
        w_side(1, 2, core).start()

        got(2, 0)
        w_side(0, 3, core).start()
        got(3, 0)
        w_side(0, 4, core).start()
        for n in range(5):
            w_side(0, n, 1 - core).wait_recv()

        for m in SENDS:
            if m not in SELF:
                for c in pieces(m):
                    t_copy(send, m, c).wait_send()

    pl.run_scoped(
        dispatch,
        pltpu.VMEM((peers - 2, padded, width), bf16),
        pltpu.VMEM((2, count, chunk), bf16),
        pltpu.VMEM((peers * padded, count), bf16))

    def finish(wown, wbuf, res, acc, pos):
        flat = jnp.concatenate(
            [pos_a, pos_b, gates[0:1, :], gates[1:2, :], jnp.zeros((124, count), f32)], axis=0)
        pos[...] = flat.T

        step = hidden // 2

        def w_load(q, n, slot):
            cols = pl.ds(n * step, step)
            return pltpu.make_async_copy(held.at[q, :, cols], wbuf.at[slot], wbsem.at[slot])

        def own_load(q):
            return pltpu.make_async_copy(held.at[q], wown.at[q], wosem.at[q])

        def own_product(base, q):
            def one(n, carry):
                cols = pl.ds(pl.multiple_of(n * step, step), step)
                left = recv[base:base + GROUP, 0:span, :].reshape(GROUP * span, width)
                prod = jnp.dot(left, wown[q, :, cols], preferred_element_type=f32).astype(bf16)
                res[base:base + GROUP, 0:span, cols] = prod.reshape(GROUP, span, step)
                return carry

            lax.fori_loop(0, hidden // step, one, 0)

        def partner_product(base, n):
            many = 2 * GROUP
            cols = slice(n * step, (n + 1) * step)
            left = recv[base:base + many, low_rows:padded, :].reshape(many * span, width)
            prod = jnp.dot(left, wbuf[n], preferred_element_type=f32).astype(bf16)
            prod = prod.reshape(many, span, step)
            edge = res[base:base + many, low_rows:low_rows + 16, cols]
            r = lax.broadcasted_iota(jnp.int32, edge.shape, 1)
            res[base:base + many, low_rows:low_rows + 16, cols] = jnp.where(
                r < cap - low_rows, edge, prod[:, 0:16])
            res[base:base + many, low_rows + 16:padded, cols] = prod[:, 16:]

        def low_copy(m):
            i = SLOTS.index(m)
            return pltpu.make_async_remote_copy(
                src_ref=res.at[i, pl.ds(0, low_rows), :], dst_ref=rr_lo.at[i],
                send_sem=lsend.at[i], recv_sem=lrecv.at[i], device_id={"exp": origin(m)})

        def high_copy(m):
            i = SLOTS.index(m)
            return pltpu.make_async_remote_copy(
                src_ref=res.at[i, pl.ds(low_rows, sent - low_rows), :],
                dst_ref=rr_hi.at[i, pl.ds(0, sent - low_rows), :],
                send_sem=hsend.at[i], recv_sem=hrecv.at[i], device_id={"exp": origin(m)})

        def arrived(m):
            if m in SELF:
                return
            if m in RELAYED:
                u_copy(m).wait_recv()
            else:
                for c in pieces(m):
                    t_copy(recv, m, c).wait_recv()

        def give_low(base):
            for i in range(base, base + GROUP):
                if SLOTS[i] in SELF:
                    rr_lo[i] = res[i, 0:low_rows, :]
                else:
                    low_copy(SLOTS[i]).start()

        def give_high(base):
            for i in range(base, base + 2 * GROUP):
                if SLOTS[i] in SELF:
                    rr_hi[i] = res[i, low_rows:padded, :]
                else:
                    high_copy(SLOTS[i]).start()

        def all_arrived(base):
            for m in SLOTS[base:base + GROUP]:
                arrived(m)

        own_load(0).start()
        own_load(1).start()
        for base, q in ((0, 0), (8, 1)):
            all_arrived(base)
            own_load(q).wait()
            own_product(base, q)
            give_low(base)

        for base, q in ((4, 0), (12, 1)):
            all_arrived(base)
            own_product(base, q)
            give_low(base)

        got(2, 1)
        w_side(1, 3, core).start()
        got(3, 1)
        w_side(1, 4, core).start()
        for n in range(5):
            w_side(1, n, 1 - core).wait_recv()

        for n in range(2):
            w_load(2, n, n).start()
        for base, q in ((0, 2), (8, 3)):
            for n in range(2):
                w_load(q, n, n).wait()
                partner_product(base, n)
                if q == 2:
                    w_load(3, n, n).start()
            give_high(base)

        slot_a, slot_b = pos[:, 0:1], pos[:, 1:2]
        gate_a, gate_b = pos[:, 2:3], pos[:, 3:4]

        def mixed(base, high):
            size = span if high else low_rows
            lane = lax.broadcasted_iota(jnp.int32, (1, GROUP * size), 1)
            target = jnp.full_like(lane, -1)
            for j in range(GROUP):
                e1, e2 = names_of(SLOTS[base + j])
                local = lane - j * size
                r = local + (low_rows if high else 0)
                value = jnp.where(r < cap, r + e1 * cap, r - cap + e2 * cap)
                target = jnp.where((local >= 0) & (local < size) & (r < rows), value, target)
            target = target.astype(f32)
            mix = jnp.where(slot_a == target, gate_a, 0.0) + jnp.where(slot_b == target, gate_b, 0.0)
            top = mix.astype(bf16)
            rest = (mix - top.astype(f32)).astype(bf16)
            for m in SLOTS[base:base + GROUP]:
                if m not in SELF:
                    (high_copy(m) if high else low_copy(m)).wait_recv()
            if high:
                right = rr_hi[base:base + GROUP]
                r = lax.broadcasted_iota(jnp.int32, right.shape, 1)
                right = jnp.where(r < rows - low_rows, right, jnp.zeros_like(right))
            else:
                right = rr_lo[base:base + GROUP]
            right = right.reshape(GROUP * size, hidden)
            return (jnp.dot(top, right, preferred_element_type=f32)
                    + jnp.dot(rest, right, preferred_element_type=f32))

        order = [(0, False), (8, False), (4, False), (12, False),
                 (0, True), (8, True), (4, True), (12, True)]
        for k, (base, high) in enumerate(order):
            part = mixed(base, high)
            if k == 0:
                acc[...] = part
            elif k < len(order) - 1:
                acc[...] += part
            else:
                out[...] = (acc[...] + part).astype(bf16)

        for m in SENDS:
            if m not in SELF:
                low_copy(m).wait_send()
                high_copy(m).wait_send()

    pl.run_scoped(
        finish,
        pltpu.VMEM((2, width, hidden), bf16),
        pltpu.VMEM((2, width, hidden // 2), bf16),
        pltpu.VMEM((peers, padded, hidden), bf16),
        pltpu.VMEM((count, hidden), f32),
        pltpu.VMEM((count, 128), f32))

    for m in RELAYED:
        u_copy(m).wait_send()
    swap(0).wait_send()
    swap(1).wait_send()
    for p in range(2):
        for copy in (w_up(p), w_down(p), w_up_far(p), w_down_far(p)):
            copy.wait_send()
        for n in range(5):
            w_side(p, n, core).wait_send()


def body(tokens, routes, gates, weights):
    peers = SIDE * SIDE
    count, width = tokens.shape
    shard, hidden = weights.shape[1:]
    cap = 5 * count // (4 * peers)
    rows = 2 * cap
    padded = -(-rows // 16) * 16
    low_rows = cap // 16 * 16
    span = padded - low_rows
    bf16 = jnp.bfloat16
    dma = pltpu.SemaphoreType.DMA
    vmem = pl.BlockSpec(memory_space=pltpu.VMEM)
    anywhere = pl.BlockSpec(memory_space=pl.ANY)
    mixed, _ = pl.pallas_call(
        functools.partial(kernel, cap),
        out_shape=(
            jax.ShapeDtypeStruct((count, hidden), bf16),
            jax.ShapeDtypeStruct((4, width, hidden), bf16),
        ),
        in_specs=[anywhere, vmem, vmem, anywhere],
        out_specs=(vmem, anywhere),
        scratch_shapes=[
            pltpu.VMEM((peers, padded, width), bf16),
            pltpu.VMEM((len(RELAYED), padded, width), bf16),
            pltpu.VMEM((peers, low_rows, hidden), bf16),
            pltpu.VMEM((peers, span, hidden), bf16),
            dma((2,)),
            dma((2,)),
            dma((2,)),
            dma((peers, 4)),
            dma((peers, 4)),
            dma((len(RELAYED),)),
            dma((len(RELAYED),)),
            dma((peers,)),
            dma((peers,)),
            dma((peers,)),
            dma((peers,)),
            dma,
            dma((22,)),
            dma((22,)),
        ],
        compiler_params=pltpu.CompilerParams(
            collective_id=0, has_side_effects=True, vmem_limit_bytes=67043328),
    )(tokens, routes.T, gates.T, weights)
    return mixed


def solution(mesh):
    if mesh.shape["exp"] != SIDE * SIDE or mesh.shape["seq"] != 2 * DEPTH:
        raise ValueError("mesh")
    return jax.shard_map(
        body,
        mesh=mesh,
        in_specs=(
            P(("seq", "exp"), None),
            P(("seq", "exp"), None),
            P(("seq", "exp"), None),
            P("exp", "seq", None),
        ),
        out_specs=P(("seq", "exp"), None),
        check_vma=False,
    )
```

time: 218 us -> 189 us (0.87)
  Pallas kernels: 208 us -> 183 us
  local copies, waits for them, and re-layouts: 5.66 us -> 2.47 us
    pallas_call x1, Pallas kernels: 208 us -> 183 us  [body(): pl.pallas_call(functools.partial(kernel, cap), out_shape=(jax.ShapeDtypeS...]
    unnamed x3 -> x1, local copies, waits for them, and re-layouts: 5.66 us -> 2.47 us
where the time goes in v3:
time: 189 us; the launch traced here: 185 us
  Pallas kernels  183 us (97%)
  local copies, waits for them, and re-layouts  2.47 us (1%)
    pallas_call x1, Pallas kernels, body(): pl.pallas_call(functools.partial(kernel, cap), out_shape=(jax.ShapeDtypeS...  183 us

profile of v3, /device:TPU:24, one launch (start us, length us, event | category | flops | bytes accessed | tf_op | source)
XLA Modules:
  0.0 185.5 jit_solution(16913805838027902297)
XLA Ops:
  0.0 183.0 %shard_map.46 = (bf16[640,1024]{1,0:T(8,128)(2,1)}, bf16[4,4096,1024]{2,1,0:T(8,128)(2,1)}) custom-call(bf16[640,4096]{1,0:T(8,128)(2,1)} %tok.1, s32[2,640]{1,0:T(2,128)} %bitcast.2, f32[2,640]{1,0:T(2,128)} %bitcast.3, bf16[2,512,1024]{2,1,0:T(8,128)(2,1)} %w.1), custom_call_target="tpu_custom_call" | custom-call | tf_op jit(solution)/shard_map/pallas_call | solution.py:477
  183.0 2.5 %copy.6 = bf16[640,1024]{1,0:T(8,128)(2,1)} copy(bf16[640,1024]{1,0:T(8,128)(2,1)} %get-tuple-element.6) | data formatting | bytes 2621440

commit v4 on v3

--- a/solution.py
+++ b/solution.py
@@ -16,6 +16,7 @@
 SLOTS = [("a", 0), ("b", 0), ("a", 2), ("a", 1), ("a", 3), ("b", 2), ("b", 1), ("b", 3),
          ("c", 0), ("d", 0), ("c", 2), ("c", 1), ("c", 3), ("d", 2), ("d", 1), ("d", 3)]
 SELF = [("a", 0), ("c", 0)]
+RING_FIRST = [("b", 1), ("d", 1)]
 RELAYED = [("b", 2), ("d", 2), ("b", 1), ("d", 1), ("b", 3), ("d", 3)]
 
 
@@ -82,6 +83,8 @@
 
     def corner(m):
         kind, d = m
+        if m in RING_FIRST:
+            return place(turn(y, d), x) if kind == "b" else place(y, turn(x, d))
         if kind == "b":
             return place(y, beside(x, turn(y, d)))
         if kind == "d":
@@ -131,8 +134,12 @@
 
     prev, after, far = turn(z, -1), turn(z, 1), turn(z, 2)
 
-    def w_copy(n, part, zz, cc, expert, many, target, mine=False):
-        dst = held.at[pl.ds(expert, many), rows_of(zz, cc), :]
+    def w_copy(n, part, zz, cc, expert, many, target, mine=False, half=None):
+        if half is None:
+            row = rows_of(zz, cc)
+        else:
+            row = pl.ds(pl.multiple_of((2 * zz + cc) * shard + half * (shard // 2), shard // 2), shard // 2)
+        dst = held.at[pl.ds(expert, many), row, :]
         return pltpu.make_async_remote_copy(
             src_ref=w if mine else dst, dst_ref=dst,
             send_sem=wsend.at[10 * part + n], recv_sem=wrecv.at[10 * part + n],
@@ -142,28 +149,38 @@
         target = place(y, mate(x, y)) if j == 0 else place(mate(y, x), x)
         return pltpu.make_async_remote_copy(
             src_ref=w.at[pl.ds(j, 1)], dst_ref=held.at[pl.ds(2 + j, 1), rows_of(z, core), :],
-            send_sem=wsend.at[20 + j], recv_sem=wrecv.at[20 + j], device_id={"exp": target})
+            send_sem=wsend.at[30 + j], recv_sem=wrecv.at[30 + j], device_id={"exp": target})
+
+    def whole(p):
+        return (0, 2) if p == 0 else (1 + p, 1)
+
+    def part_of(p, side):
+        return (side, 1, None) if p == 0 else (1 + p, 1, side)
 
     def w_up(p):
-        return w_copy(0, p, z, core, 2 * p, 2, up, mine=p == 0)
+        return w_copy(0, p, z, core, *whole(p), up, mine=p == 0)
 
     def w_down(p):
-        return w_copy(1, p, z, core, 2 * p, 2, down, mine=p == 0)
+        return w_copy(1, p, z, core, *whole(p), down, mine=p == 0)
 
     def w_up_far(p):
-        return w_copy(2, p, prev, core, 2 * p, 1, up)
+        expert, many, half = part_of(p, 0)
+        return w_copy(2, p, prev, core, expert, many, up, half=half)
 
     def w_down_far(p):
-        return w_copy(3, p, after, core, 2 * p + 1, 1, down)
+        expert, many, half = part_of(p, 1)
+        return w_copy(3, p, after, core, expert, many, down, half=half)
 
     def w_side(p, n, cc):
-        zz, expert, many = [(z, 2 * p, 2), (prev, 2 * p, 2), (after, 2 * p, 2),
-                            (far, 2 * p, 1), (far, 2 * p + 1, 1)][n]
-        return w_copy(4 + n, p, zz, cc, expert, many, sibling, mine=(p == 0 and n == 0 and cc is core))
-
-    def got(copy_n, p):
-        zz, expert, many = [(prev, 2 * p, 2), (after, 2 * p, 2), (far, 2 * p, 1), (far, 2 * p + 1, 1)][copy_n]
-        w_copy(copy_n, p, zz, core, expert, many, up).wait_recv()
+        zz = (z, prev, after, far, far)[n]
+        expert, many, half = (*whole(p), None) if n < 3 else part_of(p, n - 3)
+        return w_copy(4 + n, p, zz, cc, expert, many, sibling,
+                      mine=(p == 0 and n == 0 and cc is core), half=half)
+
+    def got(n, p):
+        zz = (prev, after, far, far)[n]
+        expert, many, half = (*whole(p), None) if n < 2 else part_of(p, n - 2)
+        w_copy(n, p, zz, core, expert, many, up, half=half).wait_recv()
 
     w_up(0).start()
     w_down(0).start()
@@ -188,7 +205,10 @@
 
     def u_copy(m):
         kind, d = m
-        target = place(turn(y, d), x) if kind == "b" else place(y, turn(x, d))
+        if m in RING_FIRST:
+            target = place(y, beside(x, y)) if kind == "b" else place(beside(y, x), x)
+        else:
+            target = place(turn(y, d), x) if kind == "b" else place(y, turn(x, d))
         i = RELAYED.index(m)
         return pltpu.make_async_remote_copy(
             src_ref=land.at[i, pl.ds(0, sent), :],
@@ -249,11 +269,11 @@
             landed(m)
             u_copy(m).start()
 
-        swap(0).wait_recv()
-        swap(1).wait_recv()
-        w_up(1).start()
-        w_down(1).start()
-        w_side(1, 0, core).start()
+        for j in range(2):
+            swap(j).wait_recv()
+            w_up(1 + j).start()
+            w_down(1 + j).start()
+            w_side(1 + j, 0, core).start()
         for m in RELAYED[:4]:
             relay(m)
         local_w.wait()
@@ -265,12 +285,13 @@
         w_side(0, 2, core).start()
         for m in RELAYED[4:]:
             relay(m)
-        got(0, 1)
-        w_up_far(1).start()
-        w_side(1, 1, core).start()
-        got(1, 1)
-        w_down_far(1).start()
-        w_side(1, 2, core).start()
+        for p in (1, 2):
+            got(0, p)
+            w_up_far(p).start()
+            w_side(p, 1, core).start()
+            got(1, p)
+            w_down_far(p).start()
+            w_side(p, 2, core).start()
 
         got(2, 0)
         w_side(0, 3, core).start()
@@ -332,12 +353,13 @@
                 src_ref=res.at[i, pl.ds(0, low_rows), :], dst_ref=rr_lo.at[i],
                 send_sem=lsend.at[i], recv_sem=lrecv.at[i], device_id={"exp": origin(m)})
 
-        def high_copy(m):
+        def high_copy(m, n):
             i = SLOTS.index(m)
+            cols = pl.ds(n * step, step)
             return pltpu.make_async_remote_copy(
-                src_ref=res.at[i, pl.ds(low_rows, sent - low_rows), :],
-                dst_ref=rr_hi.at[i, pl.ds(0, sent - low_rows), :],
-                send_sem=hsend.at[i], recv_sem=hrecv.at[i], device_id={"exp": origin(m)})
+                src_ref=res.at[i, pl.ds(low_rows, sent - low_rows), cols],
+                dst_ref=rr_hi.at[i, pl.ds(0, sent - low_rows), cols],
+                send_sem=hsend.at[i, n], recv_sem=hrecv.at[i, n], device_id={"exp": origin(m)})
 
         def arrived(m):
             if m in SELF:
@@ -349,18 +371,19 @@
                     t_copy(recv, m, c).wait_recv()
 
         def give_low(base):
-            for i in range(base, base + GROUP):
+            for i in reversed(range(base, base + GROUP)):
                 if SLOTS[i] in SELF:
                     rr_lo[i] = res[i, 0:low_rows, :]
                 else:
                     low_copy(SLOTS[i]).start()
 
-        def give_high(base):
-            for i in range(base, base + 2 * GROUP):
+        def give_high(base, n):
+            for i in reversed(range(base, base + 2 * GROUP)):
                 if SLOTS[i] in SELF:
-                    rr_hi[i] = res[i, low_rows:padded, :]
+                    cols = slice(n * step, (n + 1) * step)
+                    rr_hi[i, :, cols] = res[i, low_rows:padded, cols]
                 else:
-                    high_copy(SLOTS[i]).start()
+                    high_copy(SLOTS[i], n).start()
 
         def all_arrived(base):
             for m in SLOTS[base:base + GROUP]:
@@ -379,22 +402,31 @@
             own_product(base, q)
             give_low(base)
 
-        got(2, 1)
-        w_side(1, 3, core).start()
-        got(3, 1)
-        w_side(1, 4, core).start()
-        for n in range(5):
-            w_side(1, n, 1 - core).wait_recv()
-
+        def far_part(p):
+            got(2, p)
+            w_side(p, 3, core).start()
+            got(3, p)
+            w_side(p, 4, core).start()
+
+        def complete(p):
+            for n in range(5):
+                w_side(p, n, 1 - core).wait_recv()
+            for n in range(2):
+                w_load(1 + p, n, n).start()
+
+        far_part(1)
+        complete(1)
         for n in range(2):
-            w_load(2, n, n).start()
-        for base, q in ((0, 2), (8, 3)):
-            for n in range(2):
-                w_load(q, n, n).wait()
-                partner_product(base, n)
-                if q == 2:
-                    w_load(3, n, n).start()
-            give_high(base)
+            w_load(2, n, n).wait()
+            partner_product(0, n)
+            give_high(0, n)
+            if n == 0:
+                far_part(2)
+        complete(2)
+        for n in range(2):
+            w_load(3, n, n).wait()
+            partner_product(8, n)
+            give_high(8, n)
 
         slot_a, slot_b = pos[:, 0:1], pos[:, 1:2]
         gate_a, gate_b = pos[:, 2:3], pos[:, 3:4]
@@ -415,7 +447,8 @@
             rest = (mix - top.astype(f32)).astype(bf16)
             for m in SLOTS[base:base + GROUP]:
                 if m not in SELF:
-                    (high_copy(m) if high else low_copy(m)).wait_recv()
+                    for copy in ([high_copy(m, n) for n in range(2)] if high else [low_copy(m)]):
+                        copy.wait_recv()
             if high:
                 right = rr_hi[base:base + GROUP]
                 r = lax.broadcasted_iota(jnp.int32, right.shape, 1)
@@ -427,7 +460,7 @@
                     + jnp.dot(rest, right, preferred_element_type=f32))
 
         order = [(0, False), (8, False), (4, False), (12, False),
-                 (0, True), (8, True), (4, True), (12, True)]
+                 (4, True), (0, True), (12, True), (8, True)]
         for k, (base, high) in enumerate(order):
             part = mixed(base, high)
             if k == 0:
@@ -440,7 +473,8 @@
         for m in SENDS:
             if m not in SELF:
                 low_copy(m).wait_send()
-                high_copy(m).wait_send()
+                for n in range(2):
+                    high_copy(m, n).wait_send()
 
     pl.run_scoped(
         finish,
@@ -454,7 +488,7 @@
         u_copy(m).wait_send()
     swap(0).wait_send()
     swap(1).wait_send()
-    for p in range(2):
+    for p in range(3):
         for copy in (w_up(p), w_down(p), w_up_far(p), w_down_far(p)):
             copy.wait_send()
         for n in range(5):
@@ -496,11 +530,11 @@
             dma((len(RELAYED),)),
             dma((peers,)),
             dma((peers,)),
-            dma((peers,)),
-            dma((peers,)),
+            dma((peers, 2)),
+            dma((peers, 2)),
             dma,
-            dma((22,)),
-            dma((22,)),
+            dma((32,)),
+            dma((32,)),
         ],
         compiler_params=pltpu.CompilerParams(
             collective_id=0, has_side_effects=True, vmem_limit_bytes=67043328),

time: 189 us -> 185 us (0.979)
  Pallas kernels: 183 us -> 181 us
    pallas_call x1, Pallas kernels: 183 us -> 181 us  [body(): pl.pallas_call(functools.partial(kernel, cap), out_shape=(jax.ShapeDtypeS...]
where the time goes in v4:
time: 185 us; the launch traced here: 183 us
  Pallas kernels  181 us (98%)
  local copies, waits for them, and re-layouts  2.47 us (1%)
    pallas_call x1, Pallas kernels, body(): pl.pallas_call(functools.partial(kernel, cap), out_shape=(jax.ShapeDtypeS...  181 us

profile of v4, /device:TPU:24, one launch (start us, length us, event | category | flops | bytes accessed | tf_op | source)
XLA Modules:
  0.0 183.2 jit_solution(3794826609779715872)
XLA Ops:
  0.0 180.8 %shard_map.46 = (bf16[640,1024]{1,0:T(8,128)(2,1)}, bf16[4,4096,1024]{2,1,0:T(8,128)(2,1)}) custom-call(bf16[640,4096]{1,0:T(8,128)(2,1)} %tok.1, s32[2,640]{1,0:T(2,128)} %bitcast.2, f32[2,640]{1,0:T(2,128)} %bitcast.3, bf16[2,512,1024]{2,1,0:T(8,128)(2,1)} %w.1), custom_call_target="tpu_custom_call" | custom-call | tf_op jit(solution)/shard_map/pallas_call | solution.py:511
  180.8 2.5 %copy.6 = bf16[640,1024]{1,0:T(8,128)(2,1)} copy(bf16[640,1024]{1,0:T(8,128)(2,1)} %get-tuple-element.6) | data formatting | bytes 2621440

commit v5 on v4

--- a/solution.py
+++ b/solution.py
@@ -134,12 +134,9 @@
 
     prev, after, far = turn(z, -1), turn(z, 1), turn(z, 2)
 
-    def w_copy(n, part, zz, cc, expert, many, target, mine=False, half=None):
-        if half is None:
-            row = rows_of(zz, cc)
-        else:
-            row = pl.ds(pl.multiple_of((2 * zz + cc) * shard + half * (shard // 2), shard // 2), shard // 2)
-        dst = held.at[pl.ds(expert, many), row, :]
+    def w_copy(n, part, zz, cc, expert, many, target, mine=False):
+        cols = pl.ds(0, hidden) if part == 0 else pl.ds((part - 1) * (hidden // 2), hidden // 2)
+        dst = held.at[pl.ds(expert, many), rows_of(zz, cc), cols]
         return pltpu.make_async_remote_copy(
             src_ref=w if mine else dst, dst_ref=dst,
             send_sem=wsend.at[10 * part + n], recv_sem=wrecv.at[10 * part + n],
@@ -151,36 +148,31 @@
             src_ref=w.at[pl.ds(j, 1)], dst_ref=held.at[pl.ds(2 + j, 1), rows_of(z, core), :],
             send_sem=wsend.at[30 + j], recv_sem=wrecv.at[30 + j], device_id={"exp": target})
 
-    def whole(p):
-        return (0, 2) if p == 0 else (1 + p, 1)
-
-    def part_of(p, side):
-        return (side, 1, None) if p == 0 else (1 + p, 1, side)
+    def first_of(p):
+        return 0 if p == 0 else 2
 
     def w_up(p):
-        return w_copy(0, p, z, core, *whole(p), up, mine=p == 0)
+        return w_copy(0, p, z, core, first_of(p), 2, up, mine=p == 0)
 
     def w_down(p):
-        return w_copy(1, p, z, core, *whole(p), down, mine=p == 0)
+        return w_copy(1, p, z, core, first_of(p), 2, down, mine=p == 0)
 
     def w_up_far(p):
-        expert, many, half = part_of(p, 0)
-        return w_copy(2, p, prev, core, expert, many, up, half=half)
+        return w_copy(2, p, prev, core, first_of(p), 1, up)
 
     def w_down_far(p):
-        expert, many, half = part_of(p, 1)
-        return w_copy(3, p, after, core, expert, many, down, half=half)
+        return w_copy(3, p, after, core, first_of(p) + 1, 1, down)
 
     def w_side(p, n, cc):
         zz = (z, prev, after, far, far)[n]
-        expert, many, half = (*whole(p), None) if n < 3 else part_of(p, n - 3)
+        expert, many = first_of(p) + (n == 4), 2 if n < 3 else 1
         return w_copy(4 + n, p, zz, cc, expert, many, sibling,
-                      mine=(p == 0 and n == 0 and cc is core), half=half)
+                      mine=(p == 0 and n == 0 and cc is core))
 
     def got(n, p):
         zz = (prev, after, far, far)[n]
-        expert, many, half = (*whole(p), None) if n < 2 else part_of(p, n - 2)
-        w_copy(n, p, zz, core, expert, many, up, half=half).wait_recv()
+        expert, many = first_of(p) + (n == 3), 2 if n < 2 else 1
+        w_copy(n, p, zz, core, expert, many, up).wait_recv()
 
     w_up(0).start()
     w_down(0).start()
@@ -269,11 +261,12 @@
             landed(m)
             u_copy(m).start()
 
-        for j in range(2):
-            swap(j).wait_recv()
-            w_up(1 + j).start()
-            w_down(1 + j).start()
-            w_side(1 + j, 0, core).start()
+        swap(0).wait_recv()
+        swap(1).wait_recv()
+        for p in (1, 2):
+            w_up(p).start()
+            w_down(p).start()
+            w_side(p, 0, core).start()
         for m in RELAYED[:4]:
             relay(m)
         local_w.wait()
@@ -335,11 +328,11 @@
 
             lax.fori_loop(0, hidden // step, one, 0)
 
-        def partner_product(base, n):
+        def partner_product(base, n, slot):
             many = 2 * GROUP
             cols = slice(n * step, (n + 1) * step)
             left = recv[base:base + many, low_rows:padded, :].reshape(many * span, width)
-            prod = jnp.dot(left, wbuf[n], preferred_element_type=f32).astype(bf16)
+            prod = jnp.dot(left, wbuf[slot], preferred_element_type=f32).astype(bf16)
             prod = prod.reshape(many, span, step)
             edge = res[base:base + many, low_rows:low_rows + 16, cols]
             r = lax.broadcasted_iota(jnp.int32, edge.shape, 1)
@@ -411,27 +404,23 @@
         def complete(p):
             for n in range(5):
                 w_side(p, n, 1 - core).wait_recv()
-            for n in range(2):
-                w_load(1 + p, n, n).start()
+            for j in range(2):
+                w_load(2 + j, p - 1, j).start()
 
         far_part(1)
-        complete(1)
-        for n in range(2):
-            w_load(2, n, n).wait()
-            partner_product(0, n)
-            give_high(0, n)
-            if n == 0:
-                far_part(2)
-        complete(2)
-        for n in range(2):
-            w_load(3, n, n).wait()
-            partner_product(8, n)
-            give_high(8, n)
+        for p in (1, 2):
+            complete(p)
+            for j in range(2):
+                w_load(2 + j, p - 1, j).wait()
+                partner_product(8 * j, p - 1, j)
+                give_high(8 * j, p - 1)
+                if p == 1 and j == 0:
+                    far_part(2)
 
         slot_a, slot_b = pos[:, 0:1], pos[:, 1:2]
         gate_a, gate_b = pos[:, 2:3], pos[:, 3:4]
 
-        def mixed(base, high):
+        def mixed(k, base, high, n):
             size = span if high else low_rows
             lane = lax.broadcasted_iota(jnp.int32, (1, GROUP * size), 1)
             target = jnp.full_like(lane, -1)
@@ -447,28 +436,28 @@
             rest = (mix - top.astype(f32)).astype(bf16)
             for m in SLOTS[base:base + GROUP]:
                 if m not in SELF:
-                    for copy in ([high_copy(m, n) for n in range(2)] if high else [low_copy(m)]):
-                        copy.wait_recv()
+                    (high_copy(m, n) if high else low_copy(m)).wait_recv()
+            cols = slice(n * step, (n + 1) * step) if high else slice(0, hidden)
             if high:
-                right = rr_hi[base:base + GROUP]
+                right = rr_hi[base:base + GROUP, :, cols]
                 r = lax.broadcasted_iota(jnp.int32, right.shape, 1)
                 right = jnp.where(r < rows - low_rows, right, jnp.zeros_like(right))
             else:
                 right = rr_lo[base:base + GROUP]
-            right = right.reshape(GROUP * size, hidden)
-            return (jnp.dot(top, right, preferred_element_type=f32)
+            right = right.reshape(GROUP * size, step if high else hidden)
+            part = (jnp.dot(top, right, preferred_element_type=f32)
                     + jnp.dot(rest, right, preferred_element_type=f32))
-
-        order = [(0, False), (8, False), (4, False), (12, False),
-                 (4, True), (0, True), (12, True), (8, True)]
-        for k, (base, high) in enumerate(order):
-            part = mixed(base, high)
             if k == 0:
-                acc[...] = part
-            elif k < len(order) - 1:
-                acc[...] += part
+                acc[:, cols] = part
+            elif high and base == 8:
+                out[:, cols] = (acc[:, cols] + part).astype(bf16)
             else:
-                out[...] = (acc[...] + part).astype(bf16)
+                acc[:, cols] += part
+
+        order = [(base, False, 0) for base in (0, 8, 4, 12)]
+        order += [(base, True, n) for n in range(2) for base in (4, 0, 12, 8)]
+        for k, (base, high, n) in enumerate(order):
+            mixed(k, base, high, n)
 
         for m in SENDS:
             if m not in SELF:

time: 185 us -> 184 us (level)
  no operation moved by 1% of the time
where the time goes in v5:
time: 184 us; the launch traced here: 183 us
  Pallas kernels  180 us (98%)
  local copies, waits for them, and re-layouts  2.47 us (1%)
    pallas_call x1, Pallas kernels, body(): pl.pallas_call(functools.partial(kernel, cap), out_shape=(jax.ShapeDtypeS...  180 us

profile of v5, /device:TPU:24, one launch (start us, length us, event | category | flops | bytes accessed | tf_op | source)
XLA Modules:
  0.0 182.7 jit_solution(12615360505866107495)
XLA Ops:
  0.0 180.3 %shard_map.46 = (bf16[640,1024]{1,0:T(8,128)(2,1)}, bf16[4,4096,1024]{2,1,0:T(8,128)(2,1)}) custom-call(bf16[640,4096]{1,0:T(8,128)(2,1)} %tok.1, s32[2,640]{1,0:T(2,128)} %bitcast.2, f32[2,640]{1,0:T(2,128)} %bitcast.3, bf16[2,512,1024]{2,1,0:T(8,128)(2,1)} %w.1), custom_call_target="tpu_custom_call" | custom-call | tf_op jit(solution)/shard_map/pallas_call | solution.py:500
  180.3 2.5 %copy.6 = bf16[640,1024]{1,0:T(8,128)(2,1)} copy(bf16[640,1024]{1,0:T(8,128)(2,1)} %get-tuple-element.6) | data formatting | bytes 2621440
